TPU v7x, 32 devices: a whole 2x2x4 slice. The times are simulated.
32 devices in a mesh: pb: 2 (over x), ka: 16 (over z, y, core).
Axes of the slice: x: 2, y: 2, z: 4, core: 2. Of those that a mesh axis runs over, the one named last changes fastest.
Arguments:
- coupling: bfloat16 [2, 16, 32, 32, 384], P('pb', 'ka'), may hold values from -0.796875 to 0.796875
- phonon_occ: float32 [2, 16, 32, 12], P('pb', 'ka'), may hold values from 0.1 to 1
- band_window: int32 [2, 16, 32, 32], P('pb', 'ka'), may hold values 0 or 1
- pair_count: int32 [2, 16, 16], P('pb', 'ka'), may hold values from 0 to 2, as said below
- k_target: int32 [2, 16, 32], P('pb', 'ka'), may hold values from 0 to 127
- kq_source: int32 [2, 16, 32], P('pb', 'ka'), may hold values from 0 to 127
- velocity: float32 [3, 32, 2048], P(None, None, 'ka'), may hold values from -6 to 6
- lifetime: float32 [32, 2048], P(None, 'ka'), may hold values from 0.5 to 2
Outputs:
- deviation: float32 [3, 32, 2048], P(None, None, 'ka')
Inputs may be any that keep to these rules, and one draw needn't show every extreme that they name: pair_count[p, a, d] is the number of live tile slots among slots d * 2 to d * 2 + 1 of device (p, a); in every q-group p some owner d receives 2 live tiles from every source.
All inputs are finite; a program needn't handle non-finite values. No bound on the sum of `band_window` on one device may be relied on, other than what follows from the above.
Results may differ from a plain program's by a relative error of at most 0.012.
Values may be sent and summed in bfloat16 or wider, within the bound.
A program may use at most 64 MiB of HBM per device.

v0:
```python
import jax
import jax.numpy as jnp
from jax import lax
from jax.sharding import PartitionSpec as P

MODES = 12
TILE_SLOTS = 2
ITERS = 4


def tile_terms(weight, chosen):
    return jnp.einsum("tnm,dmt->dnt", weight, chosen, preferred_element_type=jnp.float32)


def shards(coupling, phonon_occ, band_window, pair_count, k_target, kq_source, velocity, lifetime):
    tile_count = coupling.shape[2]
    block_width = velocity.shape[2]
    directions = velocity.shape[0]
    band_count = velocity.shape[1]
    slot_live = (
        (jnp.arange(TILE_SLOTS)[None, :] < pair_count[0, 0][:, None])
        .reshape(tile_count)
        .astype(jnp.float32)
    )
    window = band_window[0, 0].astype(jnp.float32) * slot_live[:, None]
    widened = coupling[0, 0].astype(jnp.float32)
    squared = (widened * widened).reshape(tile_count, band_count, band_count, MODES)
    summed = jnp.sum(squared * phonon_occ[0, 0][:, None, None, :], axis=3)
    weight = (summed * window[:, :, None]).astype(jnp.bfloat16)
    targets = lax.all_to_all(k_target[0, 0], "ka", split_axis=0, concat_axis=0, tiled=True)
    onehot = (targets[:, None] == jnp.arange(block_width, dtype=jnp.int32)[None, :]).astype(
        jnp.float32
    )
    deviation = lifetime[None] * velocity
    for iteration in range(ITERS):
        rounded = deviation.astype(jnp.bfloat16)
        local_terms = tile_terms(weight, jnp.take(rounded, kq_source[0, 0], axis=2))
        contribution = lax.all_to_all(
            local_terms.astype(jnp.bfloat16), "ka", split_axis=2, concat_axis=2, tiled=True
        ).astype(local_terms.dtype)
        partial_value = jnp.dot(
            contribution.reshape(directions * band_count, tile_count),
            onehot,
            precision=lax.Precision.HIGHEST,
            preferred_element_type=jnp.float32,
        )
        partial_value = partial_value.reshape(directions, band_count, block_width)
        scattering = lax.psum(partial_value.astype(jnp.bfloat16), "pb").astype(jnp.float32)
        deviation = lifetime[None] * (velocity + scattering)
    return deviation


def solution(mesh):
    placed = (
        P("pb", "ka", None, None, None),
        P("pb", "ka", None, None),
        P("pb", "ka", None, None),
        P("pb", "ka", None),
        P("pb", "ka", None),
        P("pb", "ka", None),
        P(None, None, "ka"),
        P(None, "ka"),
    )
    return jax.shard_map(
        shards, mesh=mesh, in_specs=placed, out_specs=P(None, None, "ka"), check_vma=False
    )
```

profile of v0, /device:TPU:0, one launch (start us, length us, event | category | flops | bytes accessed | tf_op | source)
XLA Modules:
  0.0 100.8 jit_solution(7904888660373477923)
XLA Ops:
  0.0 0.0 copy-start.3
  0.0 0.0 copy-start.4
  0.0 0.5 broadcast.93
  0.5 1.3 %reduce.6 = s32[32]{0:T(128)S(1)} reduce(s32[1,1,32]{2,1,0:T(1,128)} %param.14, s32[]{:T(128)} %broadcast.93), dimensions={0,1}, to_apply=%param.14.reduce_sub_computation.3 | reduce | bytes 260 | tf_op args[4]
  1.9 0.7 all_to_all.19
  2.5 7.4 %all-to-all-start.1 = ((s32[16,2,1]{1,2,0:T(1,128)}), s32[16,2,1]{1,2,0:T(1,128)S(1)}, u32[]{:S(2)}, u32[]{:S(2)}) async-start(s32[16,2,1]{1,2,0:T(1,128)} %bitcast.6), calls=%async_computation.1 | async-start | bytes 16384 | tf_op jit(solution)/shard_map/all_to_all | solution.py:30
  10.0 0.7 compare_select_fusion
  10.6 0.7 compare_and_fusion
  11.3 1.3 %convert_multiply_fusion = f32[1,1,32,32,384]{4,3,2,1,0:T(8,128)S(1)} fusion(bf16[1,1,32,32,384]{4,3,2,1,0:T(8,128)(2,1)} %param.10), kind=kLoop, calls=%fused_computation.5 | loop fusion | flops 786432 | bytes 2359296 | tf_op jit(solution)/shard_map/mul | solution.py:27
  12.6 0.0 copy-start.2
  12.6 0.0 copy-start
  12.6 0.0 copy-start.1
  12.6 5.9 %copy.30 = f32[1,1,32,32,384]{3,2,4,1,0:T(8,128)} copy(f32[1,1,32,32,384]{4,3,2,1,0:T(8,128)S(1)} %convert_multiply_fusion) | data formatting | bytes 3145728 | tf_op jit(solution)/shard_map/mul | solution.py:27
  18.6 0.0 copy-done.3
  18.6 0.0 copy-done.4
  18.6 0.1 fusion.33
  18.7 0.1 reshape.74
  18.8 3.7 %multiply_reduce_fusion = f32[32,32,32]{1,0,2:T(8,128)S(1)} fusion(f32[32,32,32,12]{1,0,3,2:T(8,128)} %bitcast.43, f32[32,12]{0,1:T(8,128)S(1)} %bitcast.44), kind=kLoop, calls=%fused_computation.4 | loop fusion | flops 753664 | bytes 1705472 | tf_op jit(solution)/shard_map/reduce_sum | solution.py:28
  22.5 0.0 copy-done.2
  22.5 0.1 bitcast_multiply_fusion
  22.6 0.3 copy.31
  23.0 0.0 copy-done
  23.0 0.0 copy-done.1
  23.0 0.1 copy.29
  23.1 0.6 gather_fusion
  23.7 0.9 fusion
  24.7 0.0 all-to-all-done.1
  24.7 6.0 %all-to-all-start = ((bf16[3,32,32]{1,0,2:T(4,128)(2,1)}), bf16[3,32,32]{1,0,2:T(4,128)(2,1)S(1)}, u32[]{:S(2)}, u32[]{:S(2)}) async-start(bf16[3,32,32]{1,0,2:T(4,128)(2,1)} %fusion), calls=%async_computation | async-start | bytes 65536 | tf_op jit(solution)/shard_map/all_to_all | solution.py:38
  30.7 0.7 reduce.7
  31.4 0.1 eq.15
  31.4 5.9 %all-to-all-done = bf16[3,32,32]{1,0,2:T(4,128)(2,1)S(1)} async-done(((bf16[3,32,32]{1,0,2:T(4,128)(2,1)}), bf16[3,32,32]{1,0,2:T(4,128)(2,1)S(1)}, u32[]{:S(2)}, u32[]{:S(2)}) %all-to-all-start) | async-done | bytes 6176 | tf_op jit(solution)/shard_map/all_to_all | solution.py:38
  37.3 0.2 convolution_convert_fusion.7
  37.5 8.4 %psum.28 = bf16[3,32,128]{2,1,0:T(8,128)(2,1)S(1)} all-reduce(bf16[3,32,128]{2,1,0:T(8,128)(2,1)S(1)} %convolution_convert_fusion.7), channel_id=1, replica_groups=mesh['pb'=2,'ka'=16] {'pb'}, use_global_device_ids=true, to_apply=%region_1.0 | all-reduce | flops 12288 | bytes 49152 | tf_op jit(solution)/shard_map/psum | solution.py:48
  45.9 0.1 copy.34
  46.0 0.6 gather_fusion.1
  46.6 0.3 fusion.1
  47.0 9.2 %all_to_all.29 = bf16[3,32,32]{1,0,2:T(4,128)(2,1)S(1)} all-to-all(bf16[3,32,32]{1,0,2:T(4,128)(2,1)S(1)} %fusion.1), channel_id=1, replica_groups=mesh['pb'=2,'ka'=16] {'ka'}, dimensions={2} | all-to-all | bytes 12288 | tf_op jit(solution)/shard_map/all_to_all | solution.py:38
  56.2 0.2 convolution_convert_fusion.6
  56.3 7.2 %psum.29 = bf16[3,32,128]{2,1,0:T(8,128)(2,1)S(1)} all-reduce(bf16[3,32,128]{2,1,0:T(8,128)(2,1)S(1)} %convolution_convert_fusion.6), channel_id=1, replica_groups=mesh['pb'=2,'ka'=16] {'pb'}, use_global_device_ids=true, to_apply=%region_2.4 | all-reduce | flops 12288 | bytes 49152 | tf_op jit(solution)/shard_map/psum | solution.py:48
  63.6 0.1 copy.37
  63.8 0.6 gather_fusion.2
  64.4 0.3 fusion.2
  64.7 9.2 %all_to_all.30 = bf16[3,32,32]{1,0,2:T(4,128)(2,1)S(1)} all-to-all(bf16[3,32,32]{1,0,2:T(4,128)(2,1)S(1)} %fusion.2), channel_id=1, replica_groups=mesh['pb'=2,'ka'=16] {'ka'}, dimensions={2} | all-to-all | bytes 12288 | tf_op jit(solution)/shard_map/all_to_all | solution.py:38
  73.9 0.2 convolution_convert_fusion.5
  74.1 8.5 %psum.30 = bf16[3,32,128]{2,1,0:T(8,128)(2,1)S(1)} all-reduce(bf16[3,32,128]{2,1,0:T(8,128)(2,1)S(1)} %convolution_convert_fusion.5), channel_id=1, replica_groups=mesh['pb'=2,'ka'=16] {'pb'}, use_global_device_ids=true, to_apply=%region_3.5 | all-reduce | flops 12288 | bytes 49152 | tf_op jit(solution)/shard_map/psum | solution.py:48
  82.5 0.1 copy.40
  82.7 0.6 gather_fusion.3
  83.3 0.3 fusion.3
  83.6 9.2 %all_to_all.31 = bf16[3,32,32]{1,0,2:T(4,128)(2,1)S(1)} all-to-all(bf16[3,32,32]{1,0,2:T(4,128)(2,1)S(1)} %fusion.3), channel_id=1, replica_groups=mesh['pb'=2,'ka'=16] {'ka'}, dimensions={2} | all-to-all | bytes 12288 | tf_op jit(solution)/shard_map/all_to_all | solution.py:38
  92.8 0.2 convolution_convert_fusion.4
  93.0 7.1 %psum.31 = bf16[3,32,128]{2,1,0:T(8,128)(2,1)S(1)} all-reduce(bf16[3,32,128]{2,1,0:T(8,128)(2,1)S(1)} %convolution_convert_fusion.4), channel_id=1, replica_groups=mesh['pb'=2,'ka'=16] {'pb'}, use_global_device_ids=true, to_apply=%region_4.6 | all-reduce | flops 12288 | bytes 49152 | tf_op jit(solution)/shard_map/psum | solution.py:48
  100.1 0.6 add_multiply_fusion
  (7 shorter events, 0.1 us)
Async XLA Ops:
  0.0 18.6 %copy-start.3 = (f32[1,1,32,12]{2,1,3,0:T(1,128)S(1)}, f32[1,1,32,12]{2,1,3,0:T(1,128)}, u32[]{:S(2)}) copy-start(f32[1,1,32,12]{2,1,3,0:T(1,128)} %param.11) | copy-start | bytes 4612
  0.0 18.6 %copy-start.4 = (s32[1,1,16]{2,1,0:T(1,128)S(1)}, s32[1,1,16]{2,1,0:T(1,128)}, u32[]{:S(2)}) copy-start(s32[1,1,16]{2,1,0:T(1,128)} %param.13) | copy-start | bytes 196
  2.5 22.1 %all-to-all-start.1 = ((s32[16,2,1]{1,2,0:T(1,128)}), s32[16,2,1]{1,2,0:T(1,128)S(1)}, u32[]{:S(2)}, u32[]{:S(2)}) async-start(s32[16,2,1]{1,2,0:T(1,128)} %bitcast.6), calls=%async_computation.1 | async-start | bytes 16384 | tf_op jit(solution)/shard_map/all_to_all | solution.py:30
  12.6 9.9 %copy-start.2 = (s32[1,1,32,32]{3,2,1,0:T(8,128)S(1)}, s32[1,1,32,32]{3,2,1,0:T(8,128)}, u32[]{:S(2)}) copy-start(s32[1,1,32,32]{3,2,1,0:T(8,128)} %param.12) | copy-start | bytes 12292
  12.6 10.3 %copy-start = (f32[3,32,128]{2,1,0:T(8,128)S(1)}, f32[3,32,128]{2,1,0:T(8,128)}, u32[]{:S(2)}) copy-start(f32[3,32,128]{2,1,0:T(8,128)} %param.16) | copy-start | bytes 147460
  12.6 10.3 %copy-start.1 = (f32[32,128]{1,0:T(8,128)S(1)}, f32[32,128]{1,0:T(8,128)}, u32[]{:S(2)}) copy-start(f32[32,128]{1,0:T(8,128)} %param.17) | copy-start | bytes 49156
  24.7 12.6 %all-to-all-start = ((bf16[3,32,32]{1,0,2:T(4,128)(2,1)}), bf16[3,32,32]{1,0,2:T(4,128)(2,1)S(1)}, u32[]{:S(2)}, u32[]{:S(2)}) async-start(bf16[3,32,32]{1,0,2:T(4,128)(2,1)} %fusion), calls=%async_computation | async-start | bytes 65536 | tf_op jit(solution)/shard_map/all_to_all | solution.py:38
where the time goes:
time: 101 us
  blocking collectives  58.8 us (58%)
  starting transfers between devices  13.4 us (13%)
  local copies, waits for them, and re-layouts  10.7 us (11%)
  other arithmetic  9.2 us (9%)
  waiting for transfers between devices  5.88 us (6%)
  matrix products  2.61 us (3%)
    psum x4, blocking collectives, shards(): lax.psum(partial_value.astype(jnp.bfloat16), 'pb').astype(jnp.float32)  31.2 us
    all_to_all x3, blocking collectives, shards(): lax.all_to_all(local_terms.astype(jnp.bfloat16), 'ka', split_axis=2, conc...  27.6 us
    all_to_all x1, starting transfers between devices, shards(): lax.all_to_all(k_target[0, 0], 'ka', split_axis=0, concat_axis=0, tiled=T...  7.41 us
    all_to_all x1, starting transfers between devices, shards(): lax.all_to_all(local_terms.astype(jnp.bfloat16), 'ka', split_axis=2, conc...  6.01 us
    mul x1, local copies, waits for them, and re-layouts, shards(): widened * widened  5.94 us
    all_to_all x1, waiting for transfers between devices, shards(): lax.all_to_all(local_terms.astype(jnp.bfloat16), 'ka', split_axis=2, conc...  5.88 us
    reduce_sum x1, other arithmetic, shards(): summed = jnp.sum(squared * phonon_occ[0, 0][:, None, None, :], axis=3)  3.71 us
    gather x4, local copies, waits for them, and re-layouts, shards(): local_terms = tile_terms(weight, jnp.take(rounded, kq_source[0, 0], axis=2))  2.44 us
  transfers between devices with their start and end apart: 2, of which 1 were waited for; matrix products, arithmetic and copies ran while one was open for 15% of the time, Pallas kernels for 0%

commit v1 on v0

v1 whole, which is shorter than its diff:
```python
import functools

import jax
import jax.numpy as jnp
from jax import lax
from jax.experimental import pallas as pl
from jax.experimental.pallas import tpu as pltpu
from jax.sharding import PartitionSpec as P

ITERS = 4
LANES = 128
F32 = jnp.float32
BF16 = jnp.bfloat16


def iota(shape, axis):
    return lax.broadcasted_iota(jnp.int32, shape, axis)


def mask(condition):
    return jnp.where(condition, 1.0, 0.0)


def dot(a, b, dims=((1,), (0,)), precision=None):
    return lax.dot_general(a, b, (dims, ((), ())), precision=precision, preferred_element_type=F32)


def column(row, wanted):
    rows, width = wanted.shape
    return jnp.sum(jnp.where(wanted, jnp.broadcast_to(row, (rows, width)), 0.0), axis=1, keepdims=True)


def kernel(
    n_pb, n_ka, directions,
    coupling_hbm, occ_ref, window_ref, count_ref, target_ref, source_ref, velocity_ref, lifetime_ref,
    out_ref,
    coupling_ref, send, recv, load_sem, send_sem, recv_sem,
):
    p, a = lax.axis_index("pb"), lax.axis_index("ka")
    me = p * n_ka + a
    devices = n_pb * n_ka
    tiles, bands = window_ref.shape
    slots = tiles // n_ka
    modes = occ_ref.shape[1]
    wide = bands * modes
    width = velocity_ref.shape[1]
    row = recv.shape[-1]
    used = directions * bands
    low = 256 // bands
    span = low * bands
    groups = tiles // low

    load = pltpu.make_async_copy(coupling_hbm, coupling_ref, load_sem)
    load.start()
    barrier = pltpu.get_barrier_semaphore()

    def peer(step):
        other = lax.rem(me + step, devices)
        return {"pb": other // n_ka, "ka": lax.rem(other, n_ka)}

    def greet(step, carry):
        pl.semaphore_signal(barrier, inc=1, device_id=peer(step), device_id_type=pl.DeviceIdType.MESH)
        return carry

    lax.fori_loop(1, devices, greet, 0)

    eye = iota((tiles, tiles), 0) == iota((tiles, tiles), 1)
    owner = iota((tiles, n_ka), 0) // slots == iota((tiles, n_ka), 1)
    live = mask((iota((tiles, 1), 0) % slots).astype(F32) < column(count_ref[...].astype(F32), owner))
    source = column(source_ref[...].astype(F32), eye)
    target = column(target_ref[...].astype(F32), eye)
    pick = mask(source == iota((tiles, width), 1).astype(F32)).astype(BF16)
    target_lane = jnp.where(iota((tiles, row), 1) == used, target, 0.0)
    shown = window_ref[...].astype(F32) * live
    keep = jnp.concatenate([shown] * groups, axis=1)
    keep = jnp.where(iota((tiles, groups * bands), 1) // bands == iota((tiles, groups * bands), 0) // low, keep, 0.0)
    keep = jnp.concatenate([keep] * directions, axis=0)
    place = mask(
        (iota((tiles, directions * span), 1) % span) // bands == iota((tiles, directions * span), 0) % low
    )
    shape = (row, directions * span)
    spread = mask(
        ((iota(shape, 0) // bands) == (iota(shape, 1) // span)) & (iota(shape, 0) % bands == iota(shape, 1) % bands)
    ).astype(BF16)
    shape = (directions * groups * bands, row)
    fold = mask(
        ((iota(shape, 0) // (groups * bands)) == (iota(shape, 1) // bands))
        & (iota(shape, 0) % bands == iota(shape, 1) % bands)
    ).astype(BF16)

    pad = jnp.zeros((row - used, width), F32)
    velocity = jnp.concatenate([velocity_ref[...], pad], axis=0).T
    lifetime = jnp.concatenate([lifetime_ref[...]] * directions + [pad], axis=0).T

    shape = (modes, wide)
    occ = dot(occ_ref[...], mask(iota(shape, 1) % modes == iota(shape, 0)), precision=lax.Precision.HIGHEST)
    shape = (wide, LANES)
    start = (iota(shape, 1) % bands) * modes
    gather = mask((iota(shape, 0) >= start) & (iota(shape, 0) < start + modes)).astype(BF16)
    per = LANES // bands
    lane_block = iota((bands, LANES), 1) // bands
    load.wait()
    weight = []
    for group in range(groups):
        halves = []
        for half in range(low // per):
            total = jnp.zeros((bands, LANES), F32)
            for inner in range(per):
                tile = group * low + half * per + inner
                value = coupling_ref[tile].astype(F32)
                value = (value * value * occ[tile : tile + 1, :]).astype(BF16)
                total = jnp.where(lane_block == inner, dot(value, gather), total)
            halves.append(total)
        weight.append(jnp.concatenate(halves, axis=1))
    weight = jnp.concatenate(weight, axis=0).astype(BF16)

    deviation = lifetime * velocity
    scatter = None
    for step in range(ITERS):
        chosen = dot(pick, deviation.astype(BF16)).astype(BF16)
        chosen = (dot(chosen, spread) * place).astype(BF16)
        chosen = jnp.concatenate([chosen[:, i * span : (i + 1) * span] for i in range(directions)], axis=0)
        terms = (dot(chosen, weight, ((1,), (1,))) * keep).astype(BF16)
        terms = jnp.concatenate([terms[i * tiles : (i + 1) * tiles] for i in range(directions)], axis=1)
        terms = (dot(terms, fold) + target_lane).astype(BF16)
        send[step] = terms.reshape(n_ka, slots, row)
        if step == 0:
            pl.semaphore_wait(barrier, devices - 1)

        def post(distance, carry):
            other = lax.rem(me + distance, devices)
            pltpu.make_async_remote_copy(
                src_ref=send.at[step, lax.rem(other, n_ka)],
                dst_ref=recv.at[step, me],
                send_sem=send_sem.at[step],
                recv_sem=recv_sem.at[step],
                device_id=peer(distance),
                device_id_type=pl.DeviceIdType.MESH,
            ).start()
            return carry

        pltpu.make_async_copy(send.at[step, a], recv.at[step, me], recv_sem.at[step]).start()
        lax.fori_loop(1, devices, post, 0)
        pltpu.make_async_copy(recv.at[step], recv.at[step], recv_sem.at[step]).wait()
        arrived = recv[step].reshape(devices * slots, row)
        if scatter is None:
            shape = (devices * slots, width)
            scatter = mask(arrived[:, used : used + 1].astype(F32) == iota(shape, 1).astype(F32)).T.astype(BF16)
        deviation = lifetime * (velocity + dot(scatter, arrived))
    out_ref[...] = deviation.T[:used]
    for step in range(ITERS):
        sent = recv.at[step, pl.ds(0, devices - 1)]
        pltpu.make_async_copy(sent, sent, send_sem.at[step]).wait()


def shards(n_pb, n_ka, coupling, phonon_occ, band_window, pair_count, k_target, kq_source, velocity, lifetime):
    tiles = coupling.shape[2]
    directions, bands, width = velocity.shape
    slots = tiles // n_ka
    row = -(-(directions * bands + 1) // LANES) * LANES
    vmem = pl.BlockSpec(memory_space=pltpu.VMEM)
    out = pl.pallas_call(
        functools.partial(kernel, n_pb, n_ka, directions),
        out_shape=jax.ShapeDtypeStruct((directions * bands, width), F32),
        in_specs=[pl.BlockSpec(memory_space=pl.ANY)] + [vmem] * 7,
        out_specs=vmem,
        scratch_shapes=[
            pltpu.VMEM(coupling.shape[2:], coupling.dtype),
            pltpu.VMEM((ITERS, n_ka, slots, row), BF16),
            pltpu.VMEM((ITERS, n_pb * n_ka, slots, row), BF16),
            pltpu.SemaphoreType.DMA,
            pltpu.SemaphoreType.DMA((ITERS,)),
            pltpu.SemaphoreType.DMA((ITERS,)),
        ],
        compiler_params=pltpu.CompilerParams(collective_id=0, has_side_effects=True),
    )(
        coupling[0, 0], phonon_occ[0, 0], band_window[0, 0], pair_count[0], k_target[0], kq_source[0],
        velocity.reshape(directions * bands, width), lifetime,
    )
    return out.reshape(directions, bands, width)


def solution(mesh):
    placed = (
        P("pb", "ka", None, None, None),
        P("pb", "ka", None, None),
        P("pb", "ka", None, None),
        P("pb", "ka", None),
        P("pb", "ka", None),
        P("pb", "ka", None),
        P(None, None, "ka"),
        P(None, "ka"),
    )
    return jax.shard_map(
        functools.partial(shards, mesh.shape["pb"], mesh.shape["ka"]),
        mesh=mesh, in_specs=placed, out_specs=P(None, None, "ka"), check_vma=False,
    )
```

time: 101 us -> 32.3 us (0.32)
  blocking collectives: 58.8 us -> 0 us
  Pallas kernels: 0 us -> 29.2 us
  starting transfers between devices: 13.4 us -> 0 us
  other arithmetic: 9.2 us -> 0 us
  local copies, waits for them, and re-layouts: 10.7 us -> 2.8 us
  waiting for transfers between devices: 5.88 us -> 0 us
  matrix products: 2.61 us -> 0 us
    psum x4 -> x0, blocking collectives: 31.2 us -> none  [shards(): lax.psum(partial_value.astype(jnp.bfloat16), 'pb').astype(jnp.float32)]
    pallas_call x0 -> x1, Pallas kernels: none -> 29.2 us  [shards(): pl.pallas_call(functools.partial(kernel, n_pb, n_ka, directions), out_sha...]
    all_to_all x3 -> x0, blocking collectives: 27.6 us -> none  [shards(): lax.all_to_all(local_terms.astype(jnp.bfloat16), 'ka', split_axis=2, conc...]
    all_to_all x2 -> x0, starting transfers between devices: 13.4 us -> none  [the longest x1 7.41 us: shards(): lax.all_to_all(k_target[0, 0], 'ka', split_axis=0, concat_axis=0, tiled=T...]
    mul x1 -> x0, local copies, waits for them, and re-layouts: 5.94 us -> none  [shards(): widened * widened]
    all_to_all x2 -> x0, waiting for transfers between devices: 5.88 us -> none  [the longest x1 5.88 us: shards(): lax.all_to_all(local_terms.astype(jnp.bfloat16), 'ka', split_axis=2, conc...]
    reduce_sum x1 -> x0, other arithmetic: 3.71 us -> none  [shards(): summed = jnp.sum(squared * phonon_occ[0, 0][:, None, None, :], axis=3)]
    dot_general x8 -> x0, matrix products: 2.61 us -> none  [the longest x4 1.85 us: tile_terms(): jnp.einsum('tnm,dmt->dnt', weight, chosen, preferred_element_type=jnp.flo...]
  transfers between devices with their start and end apart: 2 -> 0, of which waited for: 1 -> 0; matrix products, arithmetic and copies ran while one was open for 15% -> 0% of each run, Pallas kernels for 0% -> 0%
where the time goes in v1:
time: 32.3 us; the launch traced here: 32 us
  Pallas kernels  29.2 us (90%)
  local copies, waits for them, and re-layouts  2.8 us (9%)
    pallas_call x1, Pallas kernels, shards(): pl.pallas_call(functools.partial(kernel, n_pb, n_ka, directions), out_sha...  29.2 us
    unnamed x4, local copies, waits for them, and re-layouts  2.8 us

profile of v1, /device:TPU:0, one launch (start us, length us, event | category | flops | bytes accessed | tf_op | source)
XLA Modules:
  0.0 32.0 jit_solution(3376616221556356414)
XLA Ops:
  0.0 0.0 copy-start
  0.0 0.7 %copy-done = f32[1,1,32,12]{2,1,3,0:T(1,128)S(1)} copy-done((f32[1,1,32,12]{2,1,3,0:T(1,128)S(1)}, f32[1,1,32,12]{2,1,3,0:T(1,128)}, u32[]{:S(2)}) %copy-start) | copy-done | bytes 1560
  0.7 0.7 %copy.9 = f32[1,1,32,12]{3,2,1,0:T(8,128)} copy(f32[1,1,32,12]{2,1,3,0:T(1,128)S(1)} %copy-done) | data formatting | bytes 3072 | tf_op args[1]
  1.4 29.2 %shard_map.82 = f32[96,128]{1,0:T(8,128)} custom-call(bf16[32,32,384]{2,1,0:T(8,128)(2,1)} %bitcast.8, f32[32,12]{1,0:T(8,128)} %bitcast.10, s32[32,32]{1,0:T(8,128)} %bitcast.12, s32[1,16]{1,0:T(1,128)} %bitcast.13, s32[1,32]{1,0:T(1,128)} %bitcast.14, s32[1,32]{1,0:T(1,128)} %bitcast.15, f32[96,128]{1,0:T(8,128)} %bitcast.11, f32[32,128]{1,0:T(8,128)} %lifetime_ref.1), custom_call_target="tpu_custom_call" | custom-call | tf_op jit(solution)/shard_map/pallas_call | solution.py:162
  30.6 1.4 %copy.11 = f32[3,32,128]{2,1,0:T(8,128)} copy(f32[3,32,128]{2,1,0:T(8,128)} %bitcast.9) | data formatting | bytes 98304
Async XLA Ops:
  0.0 0.7 %copy-start = (f32[1,1,32,12]{2,1,3,0:T(1,128)S(1)}, f32[1,1,32,12]{2,1,3,0:T(1,128)}, u32[]{:S(2)}) copy-start(f32[1,1,32,12]{2,1,3,0:T(1,128)} %param.9) | copy-start | bytes 4612

commit v2 on v1

v2 whole, which is shorter than its diff:
```python
import functools

import jax
import jax.numpy as jnp
from jax import lax
from jax.experimental import pallas as pl
from jax.experimental.pallas import tpu as pltpu
from jax.sharding import PartitionSpec as P

ITERS = 4
LANES = 128
UNROLLED = 16
F32 = jnp.float32
BF16 = jnp.bfloat16


def iota(shape, axis):
    return lax.broadcasted_iota(jnp.int32, shape, axis)


def mask(condition):
    return jnp.where(condition, 1.0, 0.0)


def dot(a, b, dims=((1,), (0,)), precision=None):
    return lax.dot_general(a, b, (dims, ((), ())), precision=precision, preferred_element_type=F32)


def column(row, wanted):
    rows, width = wanted.shape
    return jnp.sum(jnp.where(wanted, jnp.broadcast_to(row, (rows, width)), 0.0), axis=1, keepdims=True)


def each(count, act):
    if count <= 2 * UNROLLED:
        for distance in sorted(range(1, count), key=lambda d: -min(d, count - d)):
            act(distance)
    else:

        def body(distance, carry):
            act(distance)
            return carry

        lax.fori_loop(1, count, body, 0)


def kernel(
    n_pb, n_ka, directions,
    coupling_hbm, occ_ref, window_ref, count_ref, target_ref, source_ref, velocity_ref, lifetime_ref,
    out_ref,
    coupling_ref, weights, tables, send, recv, load_sem, send_sem, recv_sem, share_send, share_recv,
):
    p, a = lax.axis_index("pb"), lax.axis_index("ka")
    me = p * n_ka + a
    devices = n_pb * n_ka
    tiles, bands = window_ref.shape
    slots = tiles // n_ka
    modes = occ_ref.shape[0]
    wide = bands * modes
    width = velocity_ref.shape[1]
    row = recv.shape[-1]
    used = directions * bands
    low = 256 // bands
    span = low * bands
    groups = tiles // low

    load = pltpu.make_async_copy(coupling_hbm, coupling_ref, load_sem)
    load.start()
    barrier = pltpu.get_barrier_semaphore()

    def peer(step):
        other = lax.rem(me + step, devices)
        return {"pb": other // n_ka, "ka": lax.rem(other, n_ka)}

    def greet(distance):
        pl.semaphore_signal(barrier, inc=1, device_id=peer(distance), device_id_type=pl.DeviceIdType.MESH)

    each(devices, greet)

    eye = iota((tiles, tiles), 0) == iota((tiles, tiles), 1)
    owner = iota((tiles, n_ka), 0) // slots == iota((tiles, n_ka), 1)
    live = mask((iota((tiles, 1), 0) % slots).astype(F32) < column(count_ref[...].astype(F32), owner))
    source = column(source_ref[...].astype(F32), eye)
    target = column(target_ref[...].astype(F32), eye)
    target_lane = jnp.where(iota((tiles, row), 1) == used, target, 0.0)
    shown = window_ref[...].astype(F32) * live

    def tile_tables(shown, source):
        pick = mask(source == iota((tiles, width), 1).astype(F32)).astype(BF16)
        keep = jnp.concatenate([shown] * groups, axis=1)
        at = (tiles, groups * bands)
        keep = jnp.where(iota(at, 1) // bands == iota(at, 0) // low, keep, 0.0)
        return pick, jnp.concatenate([keep] * directions, axis=0)

    own = tile_tables(shown, source)
    tables[p] = jnp.concatenate(
        [shown, jnp.where(iota((tiles, LANES - bands), 1) == 0, source, 0.0)], axis=1
    ).astype(BF16)
    place = mask(
        (iota((tiles, directions * span), 1) % span) // bands == iota((tiles, directions * span), 0) % low
    )
    shape = (row, directions * span)
    spread = mask(
        ((iota(shape, 0) // bands) == (iota(shape, 1) // span)) & (iota(shape, 0) % bands == iota(shape, 1) % bands)
    ).astype(BF16)
    shape = (directions * groups * bands, row)
    fold = mask(
        ((iota(shape, 0) // (groups * bands)) == (iota(shape, 1) // bands))
        & (iota(shape, 0) % bands == iota(shape, 1) % bands)
    ).astype(BF16)

    pad = jnp.zeros((row - used, width), F32)
    velocity = jnp.concatenate([velocity_ref[...], pad], axis=0).T
    lifetime = jnp.concatenate([lifetime_ref[...]] * directions + [pad], axis=0).T

    shape = (modes, wide)
    occ = dot(
        occ_ref[:, 0, :], mask(iota(shape, 1) % modes == iota(shape, 0)), ((0,), (0,)), lax.Precision.HIGHEST
    )
    shape = (wide, LANES)
    start = (iota(shape, 1) % bands) * modes
    gather = mask((iota(shape, 0) >= start) & (iota(shape, 0) < start + modes)).astype(BF16)
    per = LANES // bands
    lane_block = iota((bands, LANES), 1) // bands
    load.wait()
    weight = []
    for group in range(groups):
        halves = []
        for half in range(low // per):
            total = jnp.zeros((bands, LANES), F32)
            for inner in range(per):
                tile = group * low + half * per + inner
                value = coupling_ref[tile].astype(F32)
                value = (value * value * occ[tile : tile + 1, :]).astype(BF16)
                total = jnp.where(lane_block == inner, dot(value, gather), total)
            halves.append(total)
        weight.append(jnp.concatenate(halves, axis=1))
    weight = jnp.concatenate(weight, axis=0).astype(BF16)
    weights[p] = weight

    def share(distance, held, index):
        return pltpu.make_async_remote_copy(
            src_ref=held.at[p],
            dst_ref=held.at[p],
            send_sem=share_send.at[index],
            recv_sem=share_recv.at[index],
            device_id={"pb": lax.rem(p + distance, n_pb), "ka": a},
            device_id_type=pl.DeviceIdType.MESH,
        )

    def tile_terms(chosen, pick_keep_weight):
        keep, weight = pick_keep_weight
        chosen = (dot(chosen, spread) * place).astype(BF16)
        chosen = jnp.concatenate([chosen[:, i * span : (i + 1) * span] for i in range(directions)], axis=0)
        terms = (dot(chosen, weight, ((1,), (1,))) * keep).astype(BF16)
        terms = jnp.concatenate([terms[i * tiles : (i + 1) * tiles] for i in range(directions)], axis=1)
        return dot(terms, fold)

    deviation = lifetime * velocity

    terms = tile_terms(dot(own[0], deviation.astype(BF16)).astype(BF16), (own[1], weight)) + target_lane
    send[0, 0] = terms.astype(BF16).reshape(n_ka, slots, row)
    pl.semaphore_wait(barrier, devices - 1)

    def post_all(distance):
        to = peer(distance)
        pltpu.make_async_remote_copy(
            src_ref=send.at[0, 0, to["ka"]],
            dst_ref=recv.at[0, p, a],
            send_sem=send_sem.at[0],
            recv_sem=recv_sem.at[0],
            device_id=to,
            device_id_type=pl.DeviceIdType.MESH,
        ).start()

    each(devices, post_all)
    pltpu.make_async_copy(send.at[0, 0, a], recv.at[0, p, a], recv_sem.at[0]).start()
    for distance in range(1, n_pb):
        share(distance, tables, 0).start()
        share(distance, weights, 1).start()
    for index, held in enumerate((tables, weights)):
        part = held.at[pl.ds(0, n_pb - 1)]
        pltpu.make_async_copy(part, part, share_recv.at[index]).wait()
    picks, keeps = [], []
    for q in range(n_pb):
        table = tables[q].astype(F32)
        pick, keep = tile_tables(table[:, :bands], table[:, bands : bands + 1])
        picks.append(pick)
        keeps.append(keep)
    pick = jnp.concatenate(picks, axis=0)

    def receive(step):
        pltpu.make_async_copy(recv.at[step], recv.at[step], recv_sem.at[step]).wait()
        return recv[step].reshape(devices * slots, row)

    arrived = receive(0)
    shape = (devices * slots, width)
    scatter = mask(arrived[:, used : used + 1].astype(F32) == iota(shape, 1).astype(F32)).T.astype(BF16)
    deviation = lifetime * (velocity + dot(scatter, arrived))

    for step in range(1, ITERS):
        chosen = dot(pick, deviation.astype(BF16)).astype(BF16)
        for q in range(n_pb):
            terms = tile_terms(chosen[q * tiles : (q + 1) * tiles], (keeps[q], weights[q]))
            send[step, q] = terms.astype(BF16).reshape(n_ka, slots, row)

        def post(distance):
            other = lax.rem(a + distance, n_ka)
            pltpu.make_async_remote_copy(
                src_ref=send.at[step, :, other],
                dst_ref=recv.at[step, :, a],
                send_sem=send_sem.at[step],
                recv_sem=recv_sem.at[step],
                device_id={"pb": p, "ka": other},
                device_id_type=pl.DeviceIdType.MESH,
            ).start()

        each(n_ka, post)
        pltpu.make_async_copy(send.at[step, :, a], recv.at[step, :, a], recv_sem.at[step]).start()
        deviation = lifetime * (velocity + dot(scatter, receive(step)))
    out_ref[...] = deviation.T[:used]
    for step in range(ITERS):
        if step:
            pieces = [recv.at[step, :, pl.ds(0, n_ka - 1)]]
        else:
            pieces = [recv.at[0, pl.ds(0, n_pb - 1)]] if n_pb > 1 else []
            pieces = pieces + [recv.at[0, 0, pl.ds(0, n_ka - 1)]]
        for piece in pieces:
            pltpu.make_async_copy(piece, piece, send_sem.at[step]).wait()
    for index, held in enumerate((tables, weights)):
        part = held.at[pl.ds(0, n_pb - 1)]
        pltpu.make_async_copy(part, part, share_send.at[index]).wait()


def shards(n_pb, n_ka, coupling, phonon_occ, band_window, pair_count, k_target, kq_source, velocity, lifetime):
    tiles = coupling.shape[2]
    directions, bands, width = velocity.shape
    slots = tiles // n_ka
    low = 256 // bands
    row = -(-(directions * bands + 1) // LANES) * LANES
    vmem = pl.BlockSpec(memory_space=pltpu.VMEM)
    out = pl.pallas_call(
        functools.partial(kernel, n_pb, n_ka, directions),
        out_shape=pltpu.VMEM((directions * bands, width), F32),
        in_specs=[pl.BlockSpec(memory_space=pl.ANY)] + [vmem] * 7,
        out_specs=vmem,
        scratch_shapes=[
            pltpu.VMEM(coupling.shape[2:], coupling.dtype),
            pltpu.VMEM((n_pb, tiles // low * bands, low * bands), BF16),
            pltpu.VMEM((n_pb, tiles, LANES), BF16),
            pltpu.VMEM((ITERS, n_pb, n_ka, slots, row), BF16),
            pltpu.VMEM((ITERS, n_pb, n_ka, slots, row), BF16),
            pltpu.SemaphoreType.DMA,
            pltpu.SemaphoreType.DMA((ITERS,)),
            pltpu.SemaphoreType.DMA((ITERS,)),
            pltpu.SemaphoreType.DMA((2,)),
            pltpu.SemaphoreType.DMA((2,)),
        ],
        compiler_params=pltpu.CompilerParams(collective_id=0, has_side_effects=True),
    )(
        coupling[0, 0], jnp.transpose(phonon_occ[0], (2, 0, 1)), band_window[0, 0], pair_count[0], k_target[0], kq_source[0],
        velocity.reshape(directions * bands, width), lifetime,
    )
    return out.reshape(directions, bands, width)


def solution(mesh):
    placed = (
        P("pb", "ka", None, None, None),
        P("pb", "ka", None, None),
        P("pb", "ka", None, None),
        P("pb", "ka", None),
        P("pb", "ka", None),
        P("pb", "ka", None),
        P(None, None, "ka"),
        P(None, "ka"),
    )
    return jax.shard_map(
        functools.partial(shards, mesh.shape["pb"], mesh.shape["ka"]),
        mesh=mesh, in_specs=placed, out_specs=P(None, None, "ka"), check_vma=False,
    )
```

time: 32.3 us -> 28.3 us (0.88)
  local copies, waits for them, and re-layouts: 2.8 us -> 0.62 us
  Pallas kernels: 29.2 us -> 27.4 us
    unnamed x4 -> x1, local copies, waits for them, and re-layouts: 2.8 us -> 0.62 us
    pallas_call x1, Pallas kernels: 29.2 us -> 27.4 us  [shards(): pl.pallas_call(functools.partial(kernel, n_pb, n_ka, directions), out_sha...]
where the time goes in v2:
time: 28.3 us; the launch traced here: 28 us
  Pallas kernels  27.4 us (97%)
  local copies, waits for them, and re-layouts  0.62 us (2%)
    pallas_call x1, Pallas kernels, shards(): pl.pallas_call(functools.partial(kernel, n_pb, n_ka, directions), out_sha...  27.4 us
    unnamed x1, local copies, waits for them, and re-layouts  0.62 us

profile of v2, /device:TPU:0, one launch (start us, length us, event | category | flops | bytes accessed | tf_op | source)
XLA Modules:
  0.0 28.0 jit_solution(15579873194002964593)
XLA Ops:
  0.0 27.4 %shard_map.82 = f32[96,128]{1,0:T(8,128)S(1)} custom-call(bf16[32,32,384]{2,1,0:T(8,128)(2,1)} %bitcast.11, f32[12,1,32]{2,1,0:T(1,128)} %bitcast.14, s32[32,32]{1,0:T(8,128)} %bitcast.13, s32[1,16]{1,0:T(1,128)} %bitcast.15, s32[1,32]{1,0:T(1,128)} %bitcast.16, s32[1,32]{1,0:T(1,128)} %bitcast.17, f32[96,128]{1,0:T(8,128)} %bitcast.12, f32[32,128]{1,0:T(8,128)} %lifetime_ref.1), custom_call_target="tpu_custom_call" | custom-call | tf_op jit(solution)/shard_map/pallas_call | solution.py:242
  27.4 0.6 %copy.10 = f32[3,32,128]{2,1,0:T(8,128)} copy(f32[3,32,128]{2,1,0:T(8,128)S(1)} %bitcast.10) | data formatting | bytes 98304

commit v3 on v2

--- a/solution.py
+++ b/solution.py
@@ -46,10 +46,14 @@
 
 def kernel(
     n_pb, n_ka, directions,
-    coupling_hbm, occ_ref, window_ref, count_ref, target_ref, source_ref, velocity_ref, lifetime_ref,
-    out_ref,
-    coupling_ref, weights, tables, send, recv, load_sem, send_sem, recv_sem, share_send, share_recv,
+    *refs,
 ):
+    inputs, out_ref, held = refs[:8], refs[8], refs[9:17]
+    weights, tables, send, recv, load_sem, send_sem, recv_sem, share_send, share_recv = refs[17:]
+    coupling_ref, occ_ref, window_ref, count_ref, target_ref, source_ref, velocity_ref, lifetime_ref = held
+    loads = [pltpu.make_async_copy(x, y, load_sem.at[i]) for i, (x, y) in enumerate(zip(inputs, held))]
+    for load in loads:
+        load.start()
     p, a = lax.axis_index("pb"), lax.axis_index("ka")
     me = p * n_ka + a
     devices = n_pb * n_ka
@@ -64,8 +68,6 @@
     span = low * bands
     groups = tiles // low
 
-    load = pltpu.make_async_copy(coupling_hbm, coupling_ref, load_sem)
-    load.start()
     barrier = pltpu.get_barrier_semaphore()
 
     def peer(step):
@@ -76,6 +78,8 @@
         pl.semaphore_signal(barrier, inc=1, device_id=peer(distance), device_id_type=pl.DeviceIdType.MESH)
 
     each(devices, greet)
+    for load in loads[1:]:
+        load.wait()
 
     eye = iota((tiles, tiles), 0) == iota((tiles, tiles), 1)
     owner = iota((tiles, n_ka), 0) // slots == iota((tiles, n_ka), 1)
@@ -122,7 +126,7 @@
     gather = mask((iota(shape, 0) >= start) & (iota(shape, 0) < start + modes)).astype(BF16)
     per = LANES // bands
     lane_block = iota((bands, LANES), 1) // bands
-    load.wait()
+    loads[0].wait()
     weight = []
     for group in range(groups):
         halves = []
@@ -239,28 +243,29 @@
     low = 256 // bands
     row = -(-(directions * bands + 1) // LANES) * LANES
     vmem = pl.BlockSpec(memory_space=pltpu.VMEM)
+    operands = (
+        coupling[0, 0], jnp.transpose(phonon_occ[0], (2, 0, 1)), band_window[0, 0], pair_count[0], k_target[0],
+        kq_source[0], velocity.reshape(directions * bands, width), lifetime,
+    )
     out = pl.pallas_call(
         functools.partial(kernel, n_pb, n_ka, directions),
         out_shape=pltpu.VMEM((directions * bands, width), F32),
-        in_specs=[pl.BlockSpec(memory_space=pl.ANY)] + [vmem] * 7,
+        in_specs=[pl.BlockSpec(memory_space=pl.ANY)] * len(operands),
         out_specs=vmem,
         scratch_shapes=[
-            pltpu.VMEM(coupling.shape[2:], coupling.dtype),
+            *[pltpu.VMEM(x.shape, x.dtype) for x in operands],
             pltpu.VMEM((n_pb, tiles // low * bands, low * bands), BF16),
             pltpu.VMEM((n_pb, tiles, LANES), BF16),
             pltpu.VMEM((ITERS, n_pb, n_ka, slots, row), BF16),
             pltpu.VMEM((ITERS, n_pb, n_ka, slots, row), BF16),
-            pltpu.SemaphoreType.DMA,
+            pltpu.SemaphoreType.DMA((len(operands),)),
             pltpu.SemaphoreType.DMA((ITERS,)),
             pltpu.SemaphoreType.DMA((ITERS,)),
             pltpu.SemaphoreType.DMA((2,)),
             pltpu.SemaphoreType.DMA((2,)),
         ],
         compiler_params=pltpu.CompilerParams(collective_id=0, has_side_effects=True),
-    )(
-        coupling[0, 0], jnp.transpose(phonon_occ[0], (2, 0, 1)), band_window[0, 0], pair_count[0], k_target[0], kq_source[0],
-        velocity.reshape(directions * bands, width), lifetime,
-    )
+    )(*operands)
     return out.reshape(directions, bands, width)
 
 

time: 28.3 us -> 27.6 us (0.975)
  Pallas kernels: 27.4 us -> 26.8 us
    pallas_call x1, Pallas kernels: 27.4 us -> 26.8 us  [shards(): pl.pallas_call(functools.partial(kernel, n_pb, n_ka, directions), out_sha...]
where the time goes in v3:
time: 27.6 us; the launch traced here: 27.4 us
  Pallas kernels  26.8 us (97%)
  local copies, waits for them, and re-layouts  0.62 us (2%)
    pallas_call x1, Pallas kernels, shards(): pl.pallas_call(functools.partial(kernel, n_pb, n_ka, directions), out_sha...  26.8 us
    unnamed x1, local copies, waits for them, and re-layouts  0.62 us

profile of v3, /device:TPU:0, one launch (start us, length us, event | category | flops | bytes accessed | tf_op | source)
XLA Modules:
  0.0 27.4 jit_solution(7192195512389073238)
XLA Ops:
  0.0 26.8 %shard_map.82 = f32[96,128]{1,0:T(8,128)S(1)} custom-call(bf16[32,32,384]{2,1,0:T(8,128)(2,1)} %bitcast.11, f32[12,1,32]{2,1,0:T(1,128)} %bitcast.14, s32[32,32]{1,0:T(8,128)} %bitcast.13, s32[1,16]{1,0:T(1,128)} %bitcast.15, s32[1,32]{1,0:T(1,128)} %bitcast.16, s32[1,32]{1,0:T(1,128)} %bitcast.17, f32[96,128]{1,0:T(8,128)} %bitcast.12, f32[32,128]{1,0:T(8,128)} %refs_7_.1), custom_call_target="tpu_custom_call" | custom-call | tf_op jit(solution)/shard_map/pallas_call | solution.py:250
  26.8 0.6 %copy.10 = f32[3,32,128]{2,1,0:T(8,128)} copy(f32[3,32,128]{2,1,0:T(8,128)S(1)} %bitcast.10) | data formatting | bytes 98304
